TPU v7x, 32 devices: a whole 2x2x4 slice. The times are simulated.
32 devices in a mesh: rel: 4 (over y, x), tgt: 8 (over z, core).
Axes of the slice: x: 2, y: 2, z: 4, core: 2. Of those that a mesh axis runs over, the one named last changes fastest.
Arguments:
- features: bfloat16 [2048, 768], P('tgt'), may hold values from -6 to 6
- weights: bfloat16 [8, 768, 768], P('rel'), may hold values from -0.109375 to 0.109375
- bias: float32 [768], replicated, may hold values from -3 to 3
- cotangent: bfloat16 [2048, 768], P('tgt'), may hold values from -1.0546875 to 1.0546875
- tile_values: int32 [8, 2048, 8, 128], P('rel', 'tgt'), may hold values from 0 to 3, as said below
- tile_count: int32 [8, 16], P('rel', 'tgt'), may hold values from 1 to 8, as said below
- tile_slot: int32 [8, 16, 8], P('rel', 'tgt'), may hold values from 0 to 7, as said below
- source_blocks: int32 [8, 8], replicated, may hold values from -1 to 1, as said below
Outputs:
- output: bfloat16 [2048, 768], P('tgt', 'rel')
- grad_weights: float32 [8, 768, 768], P('rel', 'tgt')
- grad_features: float32 [16, 128, 768], P('tgt', 'rel')
Inputs may be any that keep to these rules, and one draw needn't show every extreme that they name: `tile_values`: entries in tile slots at or beyond the live count are arbitrary and take no part. `tile_count`: every relation has some tile row of targets with all 8 slots live. `tile_slot`: every tile slot, live or not, names an owner for which the target block's entry of source_blocks is not -1. `source_blocks`: entry [t, o] is a block index within owner o's 2 blocks, or -1 where target block t reads nothing from o; entry [t, t] is never -1.
All inputs are finite; a program needn't handle non-finite values.
Results may differ from a plain program's by a relative error of at most 0.01.
Values may be sent and summed in bfloat16 or wider, within the bound.
A program may use at most 64 MiB of HBM per device.

v0:
```python
import jax
import jax.numpy as jnp
from jax import lax
from jax.sharding import PartitionSpec as P


def silu_pair(values):
    sigmoid = jax.nn.sigmoid(values)
    return (values * sigmoid, sigmoid * (1.0 + values * (1.0 - sigmoid)))


def padded_messages(adjacency, fetched, tile_slot):
    sources = fetched[tile_slot]
    return jnp.einsum("rqisc,rqscd->rqid", adjacency, sources, preferred_element_type=jnp.float32)


def padded_partials(adjacency, grads_blocked, tile_slot, owners):
    owner_ids = jnp.arange(owners, dtype=jnp.int32)
    summed = None
    for relation in range(adjacency.shape[0]):
        contrib = jnp.einsum(
            "qisc,qid->qscd",
            adjacency[relation],
            grads_blocked[relation],
            preferred_element_type=jnp.float32,
        )
        selector = (tile_slot[relation][..., None] == owner_ids).astype(jnp.float32)
        addend = jnp.einsum("qso,qscd->ocd", selector, contrib, precision=lax.Precision.HIGHEST)
        summed = addend if summed is None else summed + addend
    return summed


def per_device(
    features, weights, bias, cotangent, tile_values, tile_count, tile_slot, source_blocks
):
    owners = lax.axis_size("tgt")
    groups = lax.axis_size("rel")
    target_rows = features.shape[0]
    model_width = features.shape[1]
    relations = tile_values.shape[0]
    slot_total = tile_values.shape[2]
    block_rows = tile_values.shape[3]
    sections = target_rows // block_rows
    own_blocks = features.reshape(sections, block_rows, model_width)
    requested = lax.dynamic_index_in_dim(source_blocks, lax.axis_index("tgt"), 1, keepdims=False)
    listed = requested >= 0
    chosen = jnp.maximum(requested, 0)
    outgoing = jnp.where(listed[:, None, None], own_blocks[chosen], jnp.zeros((), features.dtype))
    fetched = lax.all_to_all(outgoing, "tgt", split_axis=0, concat_axis=0, tiled=True)
    live_mask = (
        jnp.arange(slot_total, dtype=jnp.int32)[None, None, :] < tile_count[:, :, None]
    ).astype(jnp.int32)
    counted = (
        tile_values.reshape(relations, sections, block_rows, slot_total, block_rows)
        * live_mask[:, :, None, :, None]
    )
    degree = jnp.sum(counted, axis=(3, 4)).astype(jnp.float32)
    adjacency = (
        counted.astype(jnp.float32) / jnp.sqrt(jnp.maximum(degree, 1.0))[..., None, None]
    ).astype(jnp.bfloat16)
    gathered_sum = padded_messages(adjacency, fetched, tile_slot)
    messages = gathered_sum.astype(jnp.bfloat16).reshape(relations, target_rows, model_width)
    partial_pre = jnp.einsum("rnd,rde->ne", messages, weights, preferred_element_type=jnp.float32)
    column_count = model_width // groups
    first_column = lax.axis_index("rel") * column_count
    preact_full = lax.psum(partial_pre, "rel") + bias
    activated, derivative_full = silu_pair(preact_full)
    output_share = lax.dynamic_slice_in_dim(activated, first_column, column_count, 1)
    grad_pre = (cotangent.astype(jnp.float32) * derivative_full).astype(jnp.bfloat16)
    output = output_share.astype(jnp.bfloat16)
    grad_messages = jnp.einsum(
        "ne,rde->rnd", grad_pre, weights, preferred_element_type=jnp.float32
    ).astype(jnp.bfloat16)
    weight_terms = jnp.einsum("rnd,ne->rde", messages, grad_pre, preferred_element_type=jnp.float32)
    grad_weights = lax.psum_scatter(weight_terms, "tgt", scatter_dimension=1, tiled=True)
    grads_blocked = grad_messages.reshape(relations, sections, block_rows, model_width)
    partials = padded_partials(adjacency, grads_blocked, tile_slot, owners)
    section_ids = jnp.arange(sections, dtype=jnp.int32)
    rounded = lax.optimization_barrier(partials.astype(jnp.bfloat16)).astype(jnp.float32)
    row_share = lax.psum_scatter(
        rounded.astype(jnp.bfloat16), "rel", scatter_dimension=1, tiled=True
    ).astype(jnp.float32)
    returned = lax.all_to_all(
        row_share.astype(jnp.bfloat16), "tgt", split_axis=0, concat_axis=0, tiled=True
    ).astype(row_share.dtype)
    matches = requested[:, None, None, None] == section_ids[None, :, None, None]
    grad_features = jnp.sum(jnp.where(matches, returned[:, None], 0.0), axis=0)
    return (output, grad_weights, grad_features)


def solution(mesh):
    placed = (
        P("tgt", None),
        P("rel", None, None),
        P(),
        P("tgt", None),
        P("rel", "tgt", None, None),
        P("rel", "tgt"),
        P("rel", "tgt", None),
        P(),
    )
    return jax.shard_map(
        per_device,
        mesh=mesh,
        in_specs=placed,
        out_specs=(P("tgt", "rel"), P("rel", "tgt", None), P("tgt", "rel", None)),
        check_vma=False,
    )
```

profile of v0, /device:TPU:0, one launch (start us, length us, event | category | flops | bytes accessed | tf_op | source)
XLA Modules:
  0.0 233.2 jit_solution(6168630421522109042)
XLA Ops:
  7.2 0.0 copy-start
  7.2 1.1 dynamic-slice_reduce_fusion
  8.2 0.0 copy-start.8
  8.3 0.5 copy-done.8
  8.8 2.8 %gather_fusion = bf16[8,128,768]{2,1,0:T(8,128)(2,1)} fusion(bf16[2,128,768]{2,1,0:T(8,128)(2,1)} %bitcast.56, s32[1024]{0:T(1024)S(1)} %pad_clamp_fusion.1), kind=kCustom, calls=%fused_computation | custom fusion | bytes 3145760 | tf_op jit(solution)/shard_map/gather | solution.py:48
  11.6 2.7 %broadcast_select_fusion = bf16[8,128,768]{2,1,0:T(8,128)(2,1)} fusion(bf16[8,128,768]{2,1,0:T(8,128)(2,1)} %gather_fusion, pred[8]{0:T(512)(128)(4,1)S(1)} %broadcast_compare_fusion), kind=kLoop, calls=%fused_computation.10 | loop fusion | flops 786432 | bytes 3145736 | tf_op jit(solution)/shard_map/jit(_where)/select_n | solution.py:48
  14.3 6.5 %all-to-all-start = ((bf16[8,128,768]{2,1,0:T(8,128)(2,1)}), bf16[8,128,768]{2,1,0:T(8,128)(2,1)}, u32[]{:S(2)}, u32[]{:S(2)}) async-start(bf16[8,128,768]{2,1,0:T(8,128)(2,1)} %broadcast_select_fusion), calls=%async_computation | async-start | bytes 3145728 | tf_op jit(solution)/shard_map/all_to_all | solution.py:49
  20.8 0.0 all-reduce.2.cloned.1.call-start
  20.8 0.0 copy-done.5
  20.9 0.1 reshape.89
  20.9 3.2 %copy.28 = s32[2,2,128,8,128]{2,3,1,4,0:T(8,128)} copy(s32[2,2,128,8,128]{4,3,2,1,0:T(8,128)} %bitcast.54) | data formatting | bytes 4194304 | tf_op jit(solution)/shard_map/reshape | solution.py:54
  24.1 0.0 copy-done.7
  24.1 0.1 compare_convert_fusion
  24.2 11.5 %multiply_reduce_fusion = s32[2,256]{1,0:T(2,128)S(1)} fusion(s32[2,256,8,128]{3,2,1,0:T(8,128)} %param.12, s32[2,256,8]{2,1,0:T(8,128)S(1)} %bitcast.59), kind=kLoop, calls=%fused_computation.7 | loop fusion | flops 1048064 | bytes 2115584 | tf_op jit(solution)/shard_map/reduce_sum | solution.py:57
  35.7 1.9 divide_convert_fusion
  37.7 0.0 copy-start.1
  37.7 21.0 %all-to-all-done = bf16[8,128,768]{2,1,0:T(8,128)(2,1)} async-done(((bf16[8,128,768]{2,1,0:T(8,128)(2,1)}), bf16[8,128,768]{2,1,0:T(8,128)(2,1)}, u32[]{:S(2)}, u32[]{:S(2)}) %all-to-all-start) | async-done | bytes 1572896 | tf_op jit(solution)/shard_map/all_to_all | solution.py:49
  58.7 5.0 %gather_fusion.1 = bf16[32,128,768]{2,1,0:T(8,128)(2,1)} fusion(bf16[8,128,768]{2,1,0:T(8,128)(2,1)} %all-to-all-done, s32[1024]{0:T(1024)S(1)} %pad_clamp_fusion), kind=kCustom, calls=%fused_computation.1 | custom fusion | bytes 12583040 | tf_op jit(solution)/shard_map/gather | solution.py:13
  63.7 0.0 copy-done.1
  63.7 6.7 %bitcast_convert_fusion = bf16[2,2,128,768]{3,2,1,0:T(8,128)(2,1)S(1)} fusion(bf16[2,2,8,128,768]{4,3,2,1,0:T(8,128)(2,1)} %bitcast.55, bf16[2,2,128,8,128]{2,3,1,4,0:T(8,128)(2,1)S(1)} %divide_convert_fusion), kind=kOutput, calls=%fused_computation.8 | convolution fusion | flops 805699584 | bytes 8126464 | tf_op jit(solution)/shard_map/rqisc,rqscd->rqid/dot_general | solution.py:14
  70.5 0.9 copy-done.3
  71.3 1.7 convolution_bitcast_fusion
  73.0 0.0 all-reduce.2.cloned.1.call-update
  73.0 0.2 reduce-scatter.5.cloned.1.call-start
  73.3 47.5 %all-reduce.2.cloned.1.call-done = f32[256,768]{1,0:T(8,128)} async-done(((f32[256,768]{1,0:T(8,128)}), f32[256,768]{1,0:T(8,128)}) %all-reduce.2.cloned.1.call-update) | async-done | bytes 786448 | tf_op jit(solution)/shard_map/psum | solution.py:66
  120.8 2.2 add_divide_fusion
  123.0 0.9 fusion.5
  123.9 0.1 fusion.21
  123.9 0.3 copy-done.2
  124.2 1.0 fusion.8
  125.2 1.0 fusion.7
  126.2 2.5 %fusion.12 = f32[8,128,768,1]{2,0,3,1:T(8,128)S(1)} fusion(f32[2,8,128,768]{3,1,0,2:T(8,128)S(1)} %fusion.8, s32[2,8]{1,0:T(2,128)S(1)} %get-tuple-element.25), kind=kOutput, calls=%fused_computation.28 | convolution fusion | flops 150995072 | bytes 9437248 | tf_op jit(solution)/shard_map/qso,qscd->ocd/dot_general | solution.py:28
  128.6 3.6 %fusion.2 = bf16[8,128,768]{2,0,1:T(8,128)(2,1)} fusion(f32[8,128,768,1]{2,0,3,1:T(8,128)S(1)} %fusion.12, f32[2,8,128,768]{3,1,0,2:T(8,128)S(1)} %fusion.7, s32[2,8]{1,0:T(2,128)S(1)} %get-tuple-element.24), kind=kOutput, calls=%fused_computation.5 | convolution fusion | flops 152567936 | bytes 11010112 | tf_op jit(solution)/shard_map/qso,qscd->ocd/dot_general | solution.py:28
  132.3 0.0 reduce-scatter.5.cloned.1.call-update
  132.3 0.0 reduce-scatter.3.cloned.1.call-start
  132.3 4.2 %fusion.19 = f32[2,768,768]{2,1,0:T(8,128)} fusion(bf16[2,256,768]{2,1,0:T(8,128)(2,1)} %bitcast.61, f32[256,768]{1,0:T(8,128)S(1)} %get-tuple-element.21, bf16[256,768]{1,0:T(8,128)(2,1)S(1)} %copy-done.4), kind=kOutput, calls=%fused_computation.43 | convolution fusion | flops 605945856 | bytes 6684672 | tf_op jit(solution)/shard_map/rnd,ne->rde/dot_general | solution.py:74
  136.5 0.0 reduce-scatter.3.cloned.1.call-update
  136.5 27.1 %reduce-scatter.5.cloned.1.call-done = bf16[8,32,768]{2,0,1:T(8,128)(2,1)} async-done(((bf16[8,128,768]{2,0,1:T(8,128)(2,1)}), bf16[8,32,768]{2,0,1:T(8,128)(2,1)}) %reduce-scatter.5.cloned.1.call-update) | async-done | bytes 393232 | tf_op jit(solution)/shard_map/reduce_scatter | solution.py:80
  163.6 1.8 copy.32
  165.4 4.6 %all-to-all-start.1 = ((bf16[8,32,768]{2,1,0:T(8,128)(2,1)}), bf16[8,32,768]{2,1,0:T(8,128)(2,1)S(1)}, u32[]{:S(2)}, u32[]{:S(2)}) async-start(bf16[8,32,768]{2,1,0:T(8,128)(2,1)} %copy.32), calls=%async_computation.3 | async-start | bytes 786432 | tf_op jit(solution)/shard_map/all_to_all | solution.py:83
  170.0 0.0 copy-done.9
  170.0 0.1 iota_compare_fusion.2
  170.1 1.9 fusion.10
  171.9 1.7 copy.33
  173.6 13.8 %all-to-all-done.1 = bf16[8,32,768]{2,1,0:T(8,128)(2,1)S(1)} async-done(((bf16[8,32,768]{2,1,0:T(8,128)(2,1)}), bf16[8,32,768]{2,1,0:T(8,128)(2,1)S(1)}, u32[]{:S(2)}, u32[]{:S(2)}) %all-to-all-start.1) | async-done | bytes 393248 | tf_op jit(solution)/shard_map/all_to_all | solution.py:83
  187.4 0.1 convert_element_type.62
  187.5 0.9 select_reduce_fusion
  188.3 38.4 %reduce-scatter.3.cloned.1.call-done = f32[2,96,768]{2,1,0:T(8,128)} async-done(((f32[2,768,768]{2,1,0:T(8,128)}), f32[2,96,768]{2,1,0:T(8,128)}) %reduce-scatter.3.cloned.1.call-update) | async-done | bytes 589840 | tf_op jit(solution)/shard_map/reduce_scatter | solution.py:75
  (18 shorter events, 0.1 us)
Async XLA Ops:
  7.2 64.2 %copy-start = (bf16[2,768,768]{2,1,0:T(8,128)(2,1)S(1)}, bf16[2,768,768]{2,1,0:T(8,128)(2,1)}, u32[]{:S(2)}) copy-start(bf16[2,768,768]{2,1,0:T(8,128)(2,1)} %param.9) | copy-start | bytes 7077892
  8.2 0.5 copy-start.8
  14.3 6.5 %copy-start.5 = (s32[2,2,8]{2,1,0:T(2,128)S(1)}, s32[2,2,8]{2,1,0:T(2,128)}, u32[]{:S(2)}) copy-start(s32[2,2,8]{2,1,0:T(2,128)} %param.14) | copy-start | bytes 388
  14.3 44.4 %all-to-all-start = ((bf16[8,128,768]{2,1,0:T(8,128)(2,1)}), bf16[8,128,768]{2,1,0:T(8,128)(2,1)}, u32[]{:S(2)}, u32[]{:S(2)}) async-start(bf16[8,128,768]{2,1,0:T(8,128)(2,1)} %broadcast_select_fusion), calls=%async_computation | async-start | bytes 3145728 | tf_op jit(solution)/shard_map/all_to_all | solution.py:49
  20.8 3.3 %copy-start.7 = (s32[2,2]{1,0:T(2,128)S(1)}, s32[2,2]{1,0:T(2,128)}, u32[]{:S(2)}) copy-start(s32[2,2]{1,0:T(2,128)} %param.13) | copy-start | bytes 52
  20.8 100.0 %all-reduce.2.cloned.1.call-start = ((), (), s32[]{:S(2)}) async-start(), calls=%async_computation.4 | async-start | bytes 1572864 | tf_op jit(solution)/shard_map/psum | solution.py:66
  37.7 26.0 %copy-start.1 = (bf16[2,2,128,8,128]{2,3,1,4,0:T(8,128)(2,1)}, bf16[2,2,128,8,128]{2,3,1,4,0:T(8,128)(2,1)S(1)}, u32[]{:S(2)}) copy-start(bf16[2,2,128,8,128]{2,3,1,4,0:T(8,128)(2,1)S(1)} %divide_convert_fusion) | copy-start | bytes 3145732
  70.4 0.9 copy-start.3
  71.3 49.4 %copy-start.6 = (f32[768]{0:T(1024)S(1)}, f32[768]{0:T(1024)}, u32[]{:S(2)}) copy-start(f32[768]{0:T(1024)} %param.10) | copy-start | bytes 9220
  73.0 50.0 %copy-start.4 = (bf16[256,768]{1,0:T(8,128)(2,1)S(1)}, bf16[256,768]{1,0:T(8,128)(2,1)}, u32[]{:S(2)}) copy-start(bf16[256,768]{1,0:T(8,128)(2,1)} %param.11) | copy-start | bytes 1179652
  73.0 90.5 %reduce-scatter.5.cloned.1.call-start = ((), (), s32[]{:S(2)}) async-start(), calls=%async_computation.6 | async-start | bytes 1966080 | tf_op jit(solution)/shard_map/reduce_scatter | solution.py:80
  123.0 1.2 copy-start.2
  132.3 94.4 %reduce-scatter.3.cloned.1.call-start = ((), (), s32[]{:S(2)}) async-start(), calls=%async_computation.5 | async-start | bytes 5308416 | tf_op jit(solution)/shard_map/reduce_scatter | solution.py:75
  136.5 33.5 %copy-start.9 = (s32[8]{0:T(128)S(1)}, s32[8]{0:T(128)}, u32[]{:S(2)}) copy-start(s32[8]{0:T(128)} %copy-done.8) | copy-start | bytes 100
  165.4 22.0 %all-to-all-start.1 = ((bf16[8,32,768]{2,1,0:T(8,128)(2,1)}), bf16[8,32,768]{2,1,0:T(8,128)(2,1)S(1)}, u32[]{:S(2)}, u32[]{:S(2)}) async-start(bf16[8,32,768]{2,1,0:T(8,128)(2,1)} %copy.32), calls=%async_computation.3 | async-start | bytes 786432 | tf_op jit(solution)/shard_map/all_to_all | solution.py:83
Sparse Core Ops, SparseCore 0:
  73.2 47.5 all-reduce.1
  132.4 31.1 reduce-scatter.4
  166.5 60.1 reduce-scatter.2
where the time goes:
time: 234 us; the launch traced here: 233 us
  waiting for transfers between devices  148 us (63%)
  other arithmetic  22.4 us (10%)
  matrix products  21.5 us (9%)
  local copies, waits for them, and re-layouts  16.3 us (7%)
  between operations  13.9 us (6%)
  starting transfers between devices  11.4 us (5%)
    psum x1, waiting for transfers between devices, per_device(): preact_full = lax.psum(partial_pre, 'rel') + bias  47.5 us
    reduce_scatter x1, waiting for transfers between devices, per_device(): lax.psum_scatter(weight_terms, 'tgt', scatter_dimension=1, tiled=True)  38.4 us
    reduce_scatter x1, waiting for transfers between devices, per_device(): lax.psum_scatter(rounded.astype(jnp.bfloat16), 'rel', scatter_dimension=1...  27.1 us
    all_to_all x1, waiting for transfers between devices, per_device(): lax.all_to_all(outgoing, 'tgt', split_axis=0, concat_axis=0, tiled=True)  21 us
    all_to_all x1, waiting for transfers between devices, per_device(): lax.all_to_all(row_share.astype(jnp.bfloat16), 'tgt', split_axis=0, conca...  13.8 us
    reduce_sum x1, other arithmetic, per_device(): degree = jnp.sum(counted, axis=(3, 4)).astype(jnp.float32)  11.5 us
    dot_general x1, matrix products, padded_messages(): jnp.einsum('rqisc,rqscd->rqid', adjacency, sources, preferred_element_typ...  6.73 us
    all_to_all x1, starting transfers between devices, per_device(): lax.all_to_all(outgoing, 'tgt', split_axis=0, concat_axis=0, tiled=True)  6.49 us
  transfers between devices with their start and end apart: 5, of which 5 were waited for; matrix products, arithmetic and copies ran while one was open for 12% of the time, Pallas kernels for 0%

commit v1 on v0

v1 whole, which is shorter than its diff:
```python
import functools

import jax
import jax.numpy as jnp
from jax import lax
from jax.experimental import pallas as pl
from jax.experimental.pallas import tpu as pltpu
from jax.sharding import PartitionSpec as P

MESH = pl.DeviceIdType.MESH
F32 = jnp.float32
BF16 = jnp.bfloat16


def aligned(start, size, multiple):
    return pl.ds(pl.multiple_of(start, multiple), size)


def is_one(condition):
    return condition.astype(jnp.int32).astype(F32)


def pack(value, first, width):
    half = value.shape[0] // 2
    return jnp.concatenate(
        [value[:half, first : first + width], value[half:, first : first + width]], axis=1
    )


def kernel(
    n, groups,
    table, counts, slots,
    feat, cot, bias, values_hbm, weights_hbm,
    out, grad_w, grad_f,
    weights, values, staged, fetched, adj, scale, msg, msg_t, pre,
    pre_send, pre_recv, gp_all, gp, gm,
    part, part_recv, part_sum, part_back,
    wg_pair, wg_pair_recv, wg_send, wg_recv,
    load_sem, a_send, a_recv, b_send, b_recv, p_send, p_recv, g_send, g_recv,
    d_send, d_recv, e_send, e_recv, w_send, w_recv, x_send, x_recv,
):
    me = lax.axis_index("tgt")
    grp = lax.axis_index("rel")
    rows, width = feat.shape
    relations = weights.shape[0]
    slot_total = slots.shape[2]
    blk = values.shape[1] // (rows * slot_total) * values.shape[2]
    sections = rows // blk
    quarter = blk // groups
    share = width // groups
    chips = n // 2
    chip, core = me // 2, lax.rem(me, 2)

    def tgt(j):
        return lax.rem(me + j, n)

    def tgt_back(j):
        return lax.rem(me + n - j, n)

    def rel(i):
        return lax.rem(grp + i, groups)

    load_w = pltpu.make_async_copy(weights_hbm, weights, load_sem.at[0])
    load_v = pltpu.make_async_copy(values_hbm, values, load_sem.at[1])
    load_v.start()
    load_w.start()

    barrier = pltpu.get_barrier_semaphore()

    @pl.loop(1, n)
    def _(j):
        pl.semaphore_signal(barrier, inc=1, device_id=(grp, tgt(j)), device_id_type=MESH)

    for i in range(1, groups):
        pl.semaphore_signal(barrier, inc=1, device_id=(rel(i), me), device_id_type=MESH)

    @pl.loop(0, n)
    def _(t):
        total = jnp.zeros((quarter, width), F32)
        for k in range(sections):
            block = feat[aligned(k * blk + grp * quarter, quarter, quarter), :].astype(F32)
            total = total + block * is_one(table[t, me] == k)
        staged[t] = total.astype(BF16)

    total = jnp.zeros((blk, width), F32)
    for k in range(sections):
        total = total + feat[k * blk : (k + 1) * blk, :].astype(F32) * is_one(table[me, me] == k)
    fetched[aligned(me * blk, blk, blk), :] = total.astype(BF16)
    pl.semaphore_wait(barrier, n - 1 + groups - 1)

    def fetch(j):
        return pltpu.make_async_remote_copy(
            src_ref=staged.at[tgt(j)],
            dst_ref=fetched.at[aligned(me * blk + grp * quarter, quarter, quarter), :],
            send_sem=a_send.at[j], recv_sem=a_recv.at[j],
            device_id=(grp, tgt(j)), device_id_type=MESH,
        )

    @pl.loop(1, n)
    def _(j):
        fetch(j).start()

    def spread(j, i):
        rows_at = aligned(tgt_back(j) * blk + grp * quarter, quarter, quarter)
        return pltpu.make_async_remote_copy(
            src_ref=fetched.at[rows_at, :], dst_ref=fetched.at[rows_at, :],
            send_sem=b_send.at[j, i], recv_sem=b_recv.at[j, i],
            device_id=(rel(i), me), device_id_type=MESH,
        )

    load_v.wait()

    @pl.loop(0, relations * sections)
    def _(b):
        r, q = b // sections, lax.rem(b, sections)
        count = counts[r, q]

        def tile(s):
            start = (q * blk * slot_total) + s
            live = (s < count).astype(jnp.int32)
            return values[r, pl.ds(start, blk, stride=slot_total), :] * live

        total = tile(0)
        for s in range(1, slot_total):
            total = total + tile(s)
        degree = jnp.sum(total.astype(F32), axis=1, keepdims=True)
        root = 1.0 / jnp.sqrt(jnp.maximum(degree, 1.0))
        scale[aligned(b * blk, blk, blk), :] = jnp.broadcast_to(root, (blk, 128))

        @pl.loop(0, n)
        def _(o):
            entry = jnp.zeros((blk, blk), jnp.int32)
            for s in range(slot_total):
                entry = entry + tile(s) * (slots[r, q, s] == o).astype(jnp.int32)
            adj[aligned(b * blk, blk, blk), aligned(o * blk, blk, blk)] = entry.astype(F32).astype(BF16)

    @pl.loop(1, n)
    def _(j):
        fetch(j).wait_recv()
        for i in range(1, groups):
            spread(j, i).start()

    load_w.wait()

    @pl.loop(1, n)
    def _(j):
        for i in range(1, groups):
            spread(j, i).wait_recv()

    for r in range(relations):
        @pl.loop(0, sections)
        def _(q):
            at = aligned(r * rows + q * blk, blk, blk)
            acc = jnp.dot(adj[at, :], fetched[...], preferred_element_type=F32)
            message = acc * scale[at, 0:1]
            msg[at, :] = message.astype(BF16)

    @pl.loop(0, sections)
    def _(q):
        total = None
        for r in range(relations):
            part_r = jnp.dot(
                msg[aligned(r * rows + q * blk, blk, blk), :], weights[r], preferred_element_type=F32
            )
            total = part_r if total is None else total + part_r
        pre[aligned(q * blk, blk, blk), :] = total

    whole = pre[...]
    for k in range(groups):
        pre_send[k] = pack(whole, k * share, share).astype(BF16)

    def reduce_pre(i):
        return pltpu.make_async_remote_copy(
            src_ref=pre_send.at[rel(i)], dst_ref=pre_recv.at[i],
            send_sem=p_send.at[i], recv_sem=p_recv.at[i],
            device_id=(rel(i), me), device_id_type=MESH,
        )

    for i in range(1, groups):
        reduce_pre(i).start()

    for r in range(relations):
        turned = msg[r * rows : (r + 1) * rows, :].astype(F32).T
        msg_t[r] = turned.reshape(n, width // n, rows).astype(BF16)

    total = pre_send[grp].astype(F32)
    for i in range(1, groups):
        reduce_pre(i).wait_recv()
        total = total + pre_recv[i].astype(F32)
    pre_act = total + bias[grp]
    sigmoid = jax.nn.sigmoid(pre_act)
    out[...] = (pre_act * sigmoid).astype(BF16)
    derivative = sigmoid * (1.0 + pre_act * (1.0 - sigmoid))
    for k in range(groups):
        @pl.when(grp == k)
        def _():
            piece = pack(cot[...].astype(F32), k * share, share)
            gp_all[k] = (piece * derivative).astype(BF16)

    def gather_gp(i):
        return pltpu.make_async_remote_copy(
            src_ref=gp_all.at[grp], dst_ref=gp_all.at[grp],
            send_sem=g_send.at[i], recv_sem=g_recv.at[i],
            device_id=(rel(i), me), device_id_type=MESH,
        )

    for i in range(1, groups):
        gather_gp(i).start()
    for i in range(1, groups):
        gather_gp(i).wait_recv()
    half = rows // 2
    for h in range(2):
        gp[h * half : (h + 1) * half, :] = jnp.concatenate(
            [gp_all[k][:, h * share : (h + 1) * share].astype(F32) for k in range(groups)], axis=1
        ).astype(BF16)

    def weight_chunk(r, t):
        return jnp.dot(msg_t[r, t], gp[...], preferred_element_type=F32)

    def pair(z):
        return pltpu.make_async_remote_copy(
            src_ref=wg_pair.at[z], dst_ref=wg_pair_recv.at[z],
            send_sem=w_send.at[z], recv_sem=w_recv.at[z],
            device_id=(grp, chip * 2 + 1 - core), device_id_type=MESH,
        )

    @pl.loop(0, chips)
    def _(z):
        for r in range(relations):
            wg_pair[z, r] = weight_chunk(r, z * 2 + 1 - core).astype(BF16)
        pair(z).start()

    def cross(j):
        z = lax.rem(chip + j, chips)
        return pltpu.make_async_remote_copy(
            src_ref=wg_send.at[j], dst_ref=wg_recv.at[j],
            send_sem=x_send.at[j], recv_sem=x_recv.at[j],
            device_id=(grp, z * 2 + core), device_id_type=MESH,
        )

    @pl.loop(0, chips)
    def _(z):
        pair(z).wait_recv()

    @pl.loop(1, chips)
    def _(j):
        z = lax.rem(chip + j, chips)
        for r in range(relations):
            summed = weight_chunk(r, z * 2 + core) + wg_pair_recv[z, r].astype(F32)
            wg_send[j, r] = summed.astype(BF16)
        cross(j).start()

    for r in range(relations):
        grad_w[r] = weight_chunk(r, me) + wg_pair_recv[chip, r].astype(F32)

    for r in range(relations):
        @pl.loop(0, sections)
        def _(q):
            at = aligned(r * rows + q * blk, blk, blk)
            grads = lax.dot_general(
                gp[aligned(q * blk, blk, blk), :], weights[r],
                (((1,), (1,)), ((), ())), preferred_element_type=F32,
            )
            gm[at, :] = (grads * scale[at, 0:1]).astype(BF16)

    def reduce_part(o, i):
        return pltpu.make_async_remote_copy(
            src_ref=part.at[o, aligned(rel(i) * quarter, quarter, quarter), :],
            dst_ref=part_recv.at[i, o],
            send_sem=d_send.at[o, i], recv_sem=d_recv.at[o, i],
            device_id=(rel(i), me), device_id_type=MESH,
        )

    @pl.loop(0, n)
    def _(j):
        o = tgt(j)
        block = lax.dot_general(
            adj[:, aligned(o * blk, blk, blk)], gm[...],
            (((0,), (0,)), ((), ())), preferred_element_type=F32,
        )
        part[o] = block.astype(BF16)
        for i in range(1, groups):
            reduce_part(o, i).start()

    def give_back(j):
        return pltpu.make_async_remote_copy(
            src_ref=part_sum.at[tgt(j)], dst_ref=part_back.at[me],
            send_sem=e_send.at[j], recv_sem=e_recv.at[j],
            device_id=(grp, tgt(j)), device_id_type=MESH,
        )

    def reduced(o):
        total = part[o, aligned(grp * quarter, quarter, quarter), :].astype(F32)
        for i in range(1, groups):
            reduce_part(o, i).wait_recv()
            total = total + part_recv[i, o].astype(F32)
        return total.astype(BF16)

    part_back[me] = reduced(me)

    @pl.loop(1, n)
    def _(j):
        part_sum[tgt(j)] = reduced(tgt(j))
        give_back(j).start()

    @pl.loop(1, chips)
    def _(j):
        cross(j).wait_recv()
        for r in range(relations):
            grad_w[r] = grad_w[r] + wg_recv[j, r].astype(F32)

    @pl.loop(1, n)
    def _(j):
        give_back(j).wait_recv()

    for k in range(sections):
        grad_f[k] = jnp.zeros((quarter, width), F32)

    @pl.loop(0, n)
    def _(t):
        wanted = table[t, me]
        addend = part_back[t].astype(F32)
        for k in range(sections):
            grad_f[k] = grad_f[k] + addend * is_one(wanted == k)

    @pl.loop(1, n)
    def _(j):
        fetch(j).wait_send()
        give_back(j).wait_send()
        for i in range(1, groups):
            spread(j, i).wait_send()

    for i in range(1, groups):
        reduce_pre(i).wait_send()
        gather_gp(i).wait_send()

    @pl.loop(0, n)
    def _(o):
        for i in range(1, groups):
            reduce_part(o, i).wait_send()

    @pl.loop(0, chips)
    def _(z):
        pair(z).wait_send()

    @pl.loop(1, chips)
    def _(j):
        cross(j).wait_send()


def per_device(
    n, groups,
    features, weights, bias, cotangent, tile_values, tile_count, tile_slot, source_blocks,
):
    rows, width = features.shape
    relations, _, slot_total, blk = tile_values.shape
    sections = rows // blk
    quarter, share, chunk, chips = blk // groups, width // groups, width // n, n // 2
    half = rows // 2
    bias_packed = jnp.tile(bias.reshape(groups, 1, share), (1, 1, 2))
    vmem = pl.BlockSpec(memory_space=pltpu.VMEM)
    smem = pl.BlockSpec(memory_space=pltpu.SMEM)
    anywhere = pl.BlockSpec(memory_space=pl.ANY)
    dma = pltpu.SemaphoreType.DMA
    out, grad_w, grad_f = pl.pallas_call(
        functools.partial(kernel, n, groups),
        out_shape=(
            jax.ShapeDtypeStruct((half, 2 * share), BF16),
            jax.ShapeDtypeStruct((relations, chunk, width), F32),
            jax.ShapeDtypeStruct((sections, quarter, width), F32),
        ),
        in_specs=[smem, smem, smem, vmem, vmem, vmem, anywhere, anywhere],
        out_specs=(vmem, vmem, vmem),
        scratch_shapes=[
            pltpu.VMEM((relations, width, width), BF16),
            pltpu.VMEM((relations, rows * slot_total, blk), jnp.int32),
            pltpu.VMEM((n, quarter, width), BF16),
            pltpu.VMEM((n * blk, width), BF16),
            pltpu.VMEM((relations * rows, n * blk), BF16),
            pltpu.VMEM((relations * rows, 128), F32),
            pltpu.VMEM((relations * rows, width), BF16),
            pltpu.VMEM((relations, n, chunk, rows), BF16),
            pltpu.VMEM((rows, width), F32),
            pltpu.VMEM((groups, half, 2 * share), BF16),
            pltpu.VMEM((groups, half, 2 * share), BF16),
            pltpu.VMEM((groups, half, 2 * share), BF16),
            pltpu.VMEM((rows, width), BF16),
            pltpu.VMEM((relations * rows, width), BF16),
            pltpu.VMEM((n, blk, width), BF16),
            pltpu.VMEM((groups, n, quarter, width), BF16),
            pltpu.VMEM((n, quarter, width), BF16),
            pltpu.VMEM((n, quarter, width), BF16),
            pltpu.VMEM((chips, relations, chunk, width), BF16),
            pltpu.VMEM((chips, relations, chunk, width), BF16),
            pltpu.VMEM((chips, relations, chunk, width), BF16),
            pltpu.VMEM((chips, relations, chunk, width), BF16),
            dma((2,)),
            dma((n,)), dma((n,)),
            dma((n, groups)), dma((n, groups)),
            dma((groups,)), dma((groups,)),
            dma((groups,)), dma((groups,)),
            dma((n, groups)), dma((n, groups)),
            dma((n,)), dma((n,)),
            dma((chips,)), dma((chips,)),
            dma((chips,)), dma((chips,)),
        ],
        compiler_params=pltpu.CompilerParams(
            collective_id=0, has_side_effects=True, vmem_limit_bytes=60 << 20
        ),
        name="layer",
    )(
        source_blocks, tile_count, tile_slot,
        features, cotangent, bias_packed,
        tile_values.reshape(relations, rows * slot_total, blk), weights,
    )
    output = out.reshape(half, 2, share).swapaxes(0, 1).reshape(rows, share)
    return (output, grad_w, grad_f)


def solution(mesh):
    placed = (
        P("tgt", None),
        P("rel", None, None),
        P(),
        P("tgt", None),
        P("rel", "tgt", None, None),
        P("rel", "tgt"),
        P("rel", "tgt", None),
        P(),
    )
    return jax.shard_map(
        functools.partial(per_device, mesh.shape["tgt"], mesh.shape["rel"]),
        mesh=mesh,
        in_specs=placed,
        out_specs=(P("tgt", "rel"), P("rel", "tgt", None), P("tgt", "rel", None)),
        check_vma=False,
    )
```

time: 234 us -> 88.2 us (0.38)
  waiting for transfers between devices: 148 us -> 0 us
  Pallas kernels: 0 us -> 80 us
  other arithmetic: 22.4 us -> 0 us
  matrix products: 21.5 us -> 0 us
  between operations: 13.9 us -> 0.65 us
  starting transfers between devices: 11.4 us -> 0 us
  local copies, waits for them, and re-layouts: 16.3 us -> 6.65 us
    pallas_call x0 -> x1, Pallas kernels: none -> 80 us  [per_device(): pl.pallas_call(functools.partial(kernel, n, groups), out_shape=(jax.Shape...]
    reduce_scatter x2 -> x0, waiting for transfers between devices: 65.4 us -> none  [the longest x1 38.4 us: per_device(): lax.psum_scatter(weight_terms, 'tgt', scatter_dimension=1, tiled=True)]
    psum x1 -> x0, waiting for transfers between devices: 47.5 us -> none  [per_device(): preact_full = lax.psum(partial_pre, 'rel') + bias]
    all_to_all x2 -> x0, waiting for transfers between devices: 34.8 us -> none  [the longest x1 21 us: per_device(): lax.all_to_all(outgoing, 'tgt', split_axis=0, concat_axis=0, tiled=True)]
    dot_general x8 -> x0, matrix products: 21.5 us -> none  [the longest x1 6.73 us: padded_messages(): jnp.einsum('rqisc,rqscd->rqid', adjacency, sources, preferred_element_typ...]
    reduce_sum x2 -> x0, other arithmetic: 12.3 us -> none  [the longest x1 11.5 us: per_device(): degree = jnp.sum(counted, axis=(3, 4)).astype(jnp.float32)]
    all_to_all x2 -> x0, starting transfers between devices: 11.1 us -> none  [the longest x1 6.49 us: per_device(): lax.all_to_all(outgoing, 'tgt', split_axis=0, concat_axis=0, tiled=True)]
    gather x2 -> x0, local copies, waits for them, and re-layouts: 7.81 us -> none  [the longest x1 5.02 us: padded_messages(): sources = fetched[tile_slot]]
  transfers between devices with their start and end apart: 5 -> 0, of which waited for: 5 -> 0; matrix products, arithmetic and copies ran while one was open for 12% -> 0% of each run, Pallas kernels for 0% -> 0%
where the time goes in v1:
time: 88.2 us; the launch traced here: 87.3 us
  Pallas kernels  80 us (91%)
  local copies, waits for them, and re-layouts  6.65 us (8%)
    pallas_call x1, Pallas kernels, per_device(): pl.pallas_call(functools.partial(kernel, n, groups), out_shape=(jax.Shape...  80 us
    unnamed x2, local copies, waits for them, and re-layouts  3.53 us

profile of v1, /device:TPU:0, one launch (start us, length us, event | category | flops | bytes accessed | tf_op | source)
XLA Modules:
  0.0 87.3 jit_solution(12361301597307411075)
XLA Ops:
  0.6 0.8 tile.10
  1.4 0.7 tile.12.bias
  2.1 80.0 %layer.1 = (bf16[128,384]{1,0:T(8,128)(2,1)}, f32[2,96,768]{2,1,0:T(8,128)}, f32[2,32,768]{2,1,0:T(8,128)}) custom-call(s32[8,8]{1,0:T(8,128)} %table.1, s32[2,2]{1,0:T(2,128)} %counts.1, s32[2,2,8]{2,1,0:T(2,128)} %slots.1, bf16[256,768]{1,0:T(8,128)(2,1)} %feat.1, bf16[256,768]{1,0:T(8,128)(2,1)} %cot.1, f32[4,1,384]{2,1,0:T(1,128)} %tile.12.bias, ...), custom_call_target="tpu_custom_call" | custom-call | tf_op jit(solution)/shard_map/layer/pallas_call | solution.py:365
  82.1 1.0 %copy.13 = bf16[128,384]{0,1:T(8,128)(2,1)S(1)} copy(bf16[128,384]{1,0:T(8,128)(2,1)} %get-tuple-element.6) | data formatting | bytes 196608 | tf_op jit(solution)/shard_map/layer/pallas_call | solution.py:365
  83.1 0.7 copy.17
  83.8 1.9 %copy.20 = f32[2,96,768]{2,1,0:T(8,128)} copy(f32[2,96,768]{2,1,0:T(8,128)} %get-tuple-element.13) | data formatting | bytes 1179648
  85.7 1.6 %copy.21 = f32[2,32,768]{2,1,0:T(8,128)} copy(f32[2,32,768]{2,1,0:T(8,128)} %get-tuple-element.14) | data formatting | bytes 393216
  (1 shorter events, 0.0 us)

commit v2 on v1

--- a/solution.py
+++ b/solution.py
@@ -32,12 +32,12 @@
     table, counts, slots,
     feat, cot, bias, values_hbm, weights_hbm,
     out, grad_w, grad_f,
-    weights, values, staged, fetched, adj, scale, msg, msg_t, pre,
-    pre_send, pre_recv, gp_all, gp, gm,
+    weights, values, staged, partner_staged, masked, fetched, adj, scale, msg, msg_t, pre,
+    pre_send, pre_recv, cot_own, bias_own, gp_all, gp, gm,
     part, part_recv, part_sum, part_back,
-    wg_pair, wg_pair_recv, wg_send, wg_recv,
+    wg_pair, wg_pair_recv, up_send, up_recv, down_send, down_recv,
     load_sem, a_send, a_recv, b_send, b_recv, p_send, p_recv, g_send, g_recv,
-    d_send, d_recv, e_send, e_recv, w_send, w_recv, x_send, x_recv,
+    d_send, d_recv, e_send, e_recv, w_send, w_recv, u_send, u_recv, v_send, v_recv,
 ):
     me = lax.axis_index("tgt")
     grp = lax.axis_index("rel")
@@ -52,10 +52,15 @@
     chip, core = me // 2, lax.rem(me, 2)
 
     def tgt(j):
-        return lax.rem(me + j, n)
+        return lax.rem(chip + j // 2, chips) * 2 + lax.rem(core + lax.rem(j, 2), 2)
 
     def tgt_back(j):
-        return lax.rem(me + n - j, n)
+        return lax.rem(chip + chips - j // 2, chips) * 2 + lax.rem(core + lax.rem(j, 2), 2)
+
+    partner = chip * 2 + 1 - core
+    row, column = grp // 2, lax.rem(grp, 2)
+    beside = row * 2 + 1 - column
+    above = (1 - row) * 2 + column
 
     def rel(i):
         return lax.rem(grp + i, groups)
@@ -82,10 +87,14 @@
             total = total + block * is_one(table[t, me] == k)
         staged[t] = total.astype(BF16)
 
-    total = jnp.zeros((blk, width), F32)
-    for k in range(sections):
-        total = total + feat[k * blk : (k + 1) * blk, :].astype(F32) * is_one(table[me, me] == k)
-    fetched[aligned(me * blk, blk, blk), :] = total.astype(BF16)
+    def whole_block(t):
+        total = jnp.zeros((blk, width), F32)
+        for k in range(sections):
+            total = total + feat[k * blk : (k + 1) * blk, :].astype(F32) * is_one(table[t, me] == k)
+        return total.astype(BF16)
+
+    fetched[aligned(me * blk, blk, blk), :] = whole_block(me)
+    partner_staged[...] = whole_block(partner)
     pl.semaphore_wait(barrier, n - 1 + groups - 1)
 
     def fetch(j):
@@ -96,17 +105,35 @@
             device_id=(grp, tgt(j)), device_id_type=MESH,
         )
 
-    @pl.loop(1, n)
+    fetch_pair = pltpu.make_async_remote_copy(
+        src_ref=partner_staged, dst_ref=fetched.at[aligned(me * blk, blk, blk), :],
+        send_sem=a_send.at[1], recv_sem=a_recv.at[1],
+        device_id=(grp, partner), device_id_type=MESH,
+    )
+
+    @pl.loop(2, n)
     def _(j):
         fetch(j).start()
 
-    def spread(j, i):
-        rows_at = aligned(tgt_back(j) * blk + grp * quarter, quarter, quarter)
+    fetch_pair.start()
+
+    def spread(j, way):
+        size = quarter if way < 2 else quarter // 2
+        source = (grp, grp, beside, above)[way]
+        extra = quarter // 2 if way == 3 else 0
+        peer = (beside, above, above, beside)[way]
+        rows_at = aligned(tgt_back(j) * blk + source * quarter + extra, size, size)
         return pltpu.make_async_remote_copy(
             src_ref=fetched.at[rows_at, :], dst_ref=fetched.at[rows_at, :],
-            send_sem=b_send.at[j, i], recv_sem=b_recv.at[j, i],
-            device_id=(rel(i), me), device_id_type=MESH,
-        )
+            send_sem=b_send.at[j, way], recv_sem=b_recv.at[j, way],
+            device_id=(peer, me), device_id_type=MESH,
+        )
+
+    def pass_on(j):
+        spread(j, 0).wait_recv()
+        spread(j, 2).start()
+        spread(j, 1).wait_recv()
+        spread(j, 3).start()
 
     load_v.wait()
 
@@ -120,9 +147,11 @@
             live = (s < count).astype(jnp.int32)
             return values[r, pl.ds(start, blk, stride=slot_total), :] * live
 
-        total = tile(0)
-        for s in range(1, slot_total):
-            total = total + tile(s)
+        total = jnp.zeros((blk, blk), jnp.int32)
+        for s in range(slot_total):
+            live_tile = tile(s)
+            masked[s] = live_tile
+            total = total + live_tile
         degree = jnp.sum(total.astype(F32), axis=1, keepdims=True)
         root = 1.0 / jnp.sqrt(jnp.maximum(degree, 1.0))
         scale[aligned(b * blk, blk, blk), :] = jnp.broadcast_to(root, (blk, 128))
@@ -131,21 +160,27 @@
         def _(o):
             entry = jnp.zeros((blk, blk), jnp.int32)
             for s in range(slot_total):
-                entry = entry + tile(s) * (slots[r, q, s] == o).astype(jnp.int32)
+                entry = entry + masked[s] * (slots[r, q, s] == o).astype(jnp.int32)
             adj[aligned(b * blk, blk, blk), aligned(o * blk, blk, blk)] = entry.astype(F32).astype(BF16)
 
-    @pl.loop(1, n)
+    @pl.loop(2, n)
     def _(j):
         fetch(j).wait_recv()
-        for i in range(1, groups):
-            spread(j, i).start()
-
+        spread(j, 0).start()
+        spread(j, 1).start()
+
+        @pl.when(j > 2)
+        def _():
+            pass_on(j - 1)
+
+    pass_on(n - 1)
     load_w.wait()
-
-    @pl.loop(1, n)
-    def _(j):
-        for i in range(1, groups):
-            spread(j, i).wait_recv()
+    fetch_pair.wait_recv()
+
+    @pl.loop(2, n)
+    def _(j):
+        spread(j, 2).wait_recv()
+        spread(j, 3).wait_recv()
 
     for r in range(relations):
         @pl.loop(0, sections)
@@ -169,45 +204,56 @@
     for k in range(groups):
         pre_send[k] = pack(whole, k * share, share).astype(BF16)
 
-    def reduce_pre(i):
-        return pltpu.make_async_remote_copy(
-            src_ref=pre_send.at[rel(i)], dst_ref=pre_recv.at[i],
-            send_sem=p_send.at[i], recv_sem=p_recv.at[i],
+    piece_rows = rows // 4
+
+    def reduce_pre(i, p):
+        at = slice(p * piece_rows, (p + 1) * piece_rows)
+        return pltpu.make_async_remote_copy(
+            src_ref=pre_send.at[rel(i), at, :], dst_ref=pre_recv.at[i, at, :],
+            send_sem=p_send.at[i, p], recv_sem=p_recv.at[i, p],
             device_id=(rel(i), me), device_id_type=MESH,
         )
 
-    for i in range(1, groups):
-        reduce_pre(i).start()
+    for p in range(2):
+        for i in range(1, groups):
+            reduce_pre(i, p).start()
 
     for r in range(relations):
         turned = msg[r * rows : (r + 1) * rows, :].astype(F32).T
         msg_t[r] = turned.reshape(n, width // n, rows).astype(BF16)
 
-    total = pre_send[grp].astype(F32)
-    for i in range(1, groups):
-        reduce_pre(i).wait_recv()
-        total = total + pre_recv[i].astype(F32)
-    pre_act = total + bias[grp]
-    sigmoid = jax.nn.sigmoid(pre_act)
-    out[...] = (pre_act * sigmoid).astype(BF16)
-    derivative = sigmoid * (1.0 + pre_act * (1.0 - sigmoid))
     for k in range(groups):
         @pl.when(grp == k)
         def _():
-            piece = pack(cot[...].astype(F32), k * share, share)
-            gp_all[k] = (piece * derivative).astype(BF16)
-
-    def gather_gp(i):
-        return pltpu.make_async_remote_copy(
-            src_ref=gp_all.at[grp], dst_ref=gp_all.at[grp],
-            send_sem=g_send.at[i], recv_sem=g_recv.at[i],
+            cot_own[...] = pack(cot[...].astype(F32), k * share, share)
+            piece = bias[:, k * share : (k + 1) * share]
+            bias_own[...] = jnp.concatenate([piece, piece], axis=1)
+
+    def gather_gp(i, p):
+        at = slice(p * piece_rows, (p + 1) * piece_rows)
+        return pltpu.make_async_remote_copy(
+            src_ref=gp_all.at[grp, at, :], dst_ref=gp_all.at[grp, at, :],
+            send_sem=g_send.at[i, p], recv_sem=g_recv.at[i, p],
             device_id=(rel(i), me), device_id_type=MESH,
         )
 
-    for i in range(1, groups):
-        gather_gp(i).start()
-    for i in range(1, groups):
-        gather_gp(i).wait_recv()
+    for p in range(2):
+        at = slice(p * piece_rows, (p + 1) * piece_rows)
+        total = pre_send[grp, at, :].astype(F32)
+        for i in range(1, groups):
+            reduce_pre(i, p).wait_recv()
+            total = total + pre_recv[i, at, :].astype(F32)
+        pre_act = total + bias_own[...]
+        sigmoid = jax.nn.sigmoid(pre_act)
+        derivative = sigmoid * (1.0 + pre_act * (1.0 - sigmoid))
+        gp_all[grp, at, :] = (cot_own[at, :] * derivative).astype(BF16)
+        for i in range(1, groups):
+            gather_gp(i, p).start()
+        out[at, :] = (pre_act * sigmoid).astype(BF16)
+
+    for p in range(2):
+        for i in range(1, groups):
+            gather_gp(i, p).wait_recv()
     half = rows // 2
     for h in range(2):
         gp[h * half : (h + 1) * half, :] = jnp.concatenate(
@@ -221,7 +267,7 @@
         return pltpu.make_async_remote_copy(
             src_ref=wg_pair.at[z], dst_ref=wg_pair_recv.at[z],
             send_sem=w_send.at[z], recv_sem=w_recv.at[z],
-            device_id=(grp, chip * 2 + 1 - core), device_id_type=MESH,
+            device_id=(grp, partner), device_id_type=MESH,
         )
 
     @pl.loop(0, chips)
@@ -230,28 +276,63 @@
             wg_pair[z, r] = weight_chunk(r, z * 2 + 1 - core).astype(BF16)
         pair(z).start()
 
-    def cross(j):
-        z = lax.rem(chip + j, chips)
-        return pltpu.make_async_remote_copy(
-            src_ref=wg_send.at[j], dst_ref=wg_recv.at[j],
-            send_sem=x_send.at[j], recv_sem=x_recv.at[j],
-            device_id=(grp, z * 2 + core), device_id_type=MESH,
-        )
+    def climb(d):
+        return pltpu.make_async_remote_copy(
+            src_ref=up_send.at[d], dst_ref=up_recv.at[d],
+            send_sem=u_send.at[d], recv_sem=u_recv.at[d],
+            device_id=(grp, jnp.minimum(chip + 1, chips - 1) * 2 + core), device_id_type=MESH,
+        )
+
+    def descend(d):
+        return pltpu.make_async_remote_copy(
+            src_ref=down_send.at[d], dst_ref=down_recv.at[d],
+            send_sem=v_send.at[d], recv_sem=v_recv.at[d],
+            device_id=(grp, jnp.maximum(chip - 1, 0) * 2 + core), device_id_type=MESH,
+        )
+
+    def chip_sum(r, z):
+        return weight_chunk(r, z * 2 + core) + wg_pair_recv[z, r].astype(F32)
+
+    def line_step(step):
+        @pl.when(step >= chip)
+        def _():
+            d = chips - 1 - step + chip
+
+            @pl.when(chip > 0)
+            def _():
+                climb(d).wait_recv()
+                for r in range(relations):
+                    up_send[d, r] = (chip_sum(r, d) + up_recv[d, r].astype(F32)).astype(BF16)
+
+            @pl.when(chip == 0)
+            def _():
+                for r in range(relations):
+                    up_send[d, r] = chip_sum(r, d).astype(BF16)
+
+            climb(d).start()
+
+        @pl.when(step >= chips - 1 - chip)
+        def _():
+            d = step - chips + 1 + chip
+
+            @pl.when(chip < chips - 1)
+            def _():
+                descend(d).wait_recv()
+                for r in range(relations):
+                    down_send[d, r] = (chip_sum(r, d) + down_recv[d, r].astype(F32)).astype(BF16)
+
+            @pl.when(chip == chips - 1)
+            def _():
+                for r in range(relations):
+                    down_send[d, r] = chip_sum(r, d).astype(BF16)
+
+            descend(d).start()
 
     @pl.loop(0, chips)
     def _(z):
         pair(z).wait_recv()
 
-    @pl.loop(1, chips)
-    def _(j):
-        z = lax.rem(chip + j, chips)
-        for r in range(relations):
-            summed = weight_chunk(r, z * 2 + core) + wg_pair_recv[z, r].astype(F32)
-            wg_send[j, r] = summed.astype(BF16)
-        cross(j).start()
-
-    for r in range(relations):
-        grad_w[r] = weight_chunk(r, me) + wg_pair_recv[chip, r].astype(F32)
+    line_step(0)
 
     for r in range(relations):
         @pl.loop(0, sections)
@@ -282,6 +363,13 @@
         for i in range(1, groups):
             reduce_part(o, i).start()
 
+    @pl.loop(1, chips - 1)
+    def _(step):
+        line_step(step)
+
+    for r in range(relations):
+        grad_w[r] = chip_sum(r, chip)
+
     def give_back(j):
         return pltpu.make_async_remote_copy(
             src_ref=part_sum.at[tgt(j)], dst_ref=part_back.at[me],
@@ -303,11 +391,17 @@
         part_sum[tgt(j)] = reduced(tgt(j))
         give_back(j).start()
 
-    @pl.loop(1, chips)
-    def _(j):
-        cross(j).wait_recv()
+    @pl.when(chip > 0)
+    def _():
+        climb(chip).wait_recv()
         for r in range(relations):
-            grad_w[r] = grad_w[r] + wg_recv[j, r].astype(F32)
+            grad_w[r] = grad_w[r] + up_recv[chip, r].astype(F32)
+
+    @pl.when(chip < chips - 1)
+    def _():
+        descend(chip).wait_recv()
+        for r in range(relations):
+            grad_w[r] = grad_w[r] + down_recv[chip, r].astype(F32)
 
     @pl.loop(1, n)
     def _(j):
@@ -323,16 +417,22 @@
         for k in range(sections):
             grad_f[k] = grad_f[k] + addend * is_one(wanted == k)
 
+    fetch_pair.wait_send()
+
+    @pl.loop(2, n)
+    def _(j):
+        fetch(j).wait_send()
+        for way in range(4):
+            spread(j, way).wait_send()
+
     @pl.loop(1, n)
     def _(j):
-        fetch(j).wait_send()
         give_back(j).wait_send()
-        for i in range(1, groups):
-            spread(j, i).wait_send()
 
     for i in range(1, groups):
-        reduce_pre(i).wait_send()
-        gather_gp(i).wait_send()
+        for p in range(2):
+            reduce_pre(i, p).wait_send()
+            gather_gp(i, p).wait_send()
 
     @pl.loop(0, n)
     def _(o):
@@ -343,9 +443,13 @@
     def _(z):
         pair(z).wait_send()
 
-    @pl.loop(1, chips)
-    def _(j):
-        cross(j).wait_send()
+        @pl.when(z > chip)
+        def _():
+            climb(z).wait_send()
+
+        @pl.when(z < chip)
+        def _():
+            descend(z).wait_send()
 
 
 def per_device(
@@ -357,7 +461,6 @@
     sections = rows // blk
     quarter, share, chunk, chips = blk // groups, width // groups, width // n, n // 2
     half = rows // 2
-    bias_packed = jnp.tile(bias.reshape(groups, 1, share), (1, 1, 2))
     vmem = pl.BlockSpec(memory_space=pltpu.VMEM)
     smem = pl.BlockSpec(memory_space=pltpu.SMEM)
     anywhere = pl.BlockSpec(memory_space=pl.ANY)
@@ -375,6 +478,8 @@
             pltpu.VMEM((relations, width, width), BF16),
             pltpu.VMEM((relations, rows * slot_total, blk), jnp.int32),
             pltpu.VMEM((n, quarter, width), BF16),
+            pltpu.VMEM((blk, width), BF16),
+            pltpu.VMEM((slot_total, blk, blk), jnp.int32),
             pltpu.VMEM((n * blk, width), BF16),
             pltpu.VMEM((relations * rows, n * blk), BF16),
             pltpu.VMEM((relations * rows, 128), F32),
@@ -383,6 +488,8 @@
             pltpu.VMEM((rows, width), F32),
             pltpu.VMEM((groups, half, 2 * share), BF16),
             pltpu.VMEM((groups, half, 2 * share), BF16),
+            pltpu.VMEM((half, 2 * share), F32),
+            pltpu.VMEM((1, 2 * share), F32),
             pltpu.VMEM((groups, half, 2 * share), BF16),
             pltpu.VMEM((rows, width), BF16),
             pltpu.VMEM((relations * rows, width), BF16),
@@ -394,13 +501,16 @@
             pltpu.VMEM((chips, relations, chunk, width), BF16),
             pltpu.VMEM((chips, relations, chunk, width), BF16),
             pltpu.VMEM((chips, relations, chunk, width), BF16),
+            pltpu.VMEM((chips, relations, chunk, width), BF16),
+            pltpu.VMEM((chips, relations, chunk, width), BF16),
             dma((2,)),
             dma((n,)), dma((n,)),
-            dma((n, groups)), dma((n, groups)),
-            dma((groups,)), dma((groups,)),
-            dma((groups,)), dma((groups,)),
+            dma((n, 4)), dma((n, 4)),
+            dma((groups, 2)), dma((groups, 2)),
+            dma((groups, 2)), dma((groups, 2)),
             dma((n, groups)), dma((n, groups)),
             dma((n,)), dma((n,)),
+            dma((chips,)), dma((chips,)),
             dma((chips,)), dma((chips,)),
             dma((chips,)), dma((chips,)),
         ],
@@ -410,7 +520,7 @@
         name="layer",
     )(
         source_blocks, tile_count, tile_slot,
-        features, cotangent, bias_packed,
+        features, cotangent, bias.reshape(1, width),
         tile_values.reshape(relations, rows * slot_total, blk), weights,
     )
     output = out.reshape(half, 2, share).swapaxes(0, 1).reshape(rows, share)

time: 88.2 us -> 84.5 us (0.958)
  Pallas kernels: 80 us -> 77.1 us
    pallas_call x1, Pallas kernels: 80 us -> 77.1 us  [per_device(): pl.pallas_call(functools.partial(kernel, n, groups), out_shape=(jax.Shape...]
    another operation x3 -> x0, local copies, waits for them, and re-layouts: 1.45 us -> none  [per_device(): bias_packed = jnp.tile(bias.reshape(groups, 1, share), (1, 1, 2))]
    reshape x0 -> x1, local copies, waits for them, and re-layouts: none -> 1.27 us  [per_device(): bias.reshape(1, width)]
where the time goes in v2:
time: 84.5 us; the launch traced here: 84.2 us
  Pallas kernels  77.1 us (91%)
  local copies, waits for them, and re-layouts  6.47 us (8%)
    pallas_call x1, Pallas kernels, per_device(): pl.pallas_call(functools.partial(kernel, n, groups), out_shape=(jax.Shape...  77.1 us
    unnamed x2, local copies, waits for them, and re-layouts  3.53 us

profile of v2, /device:TPU:0, one launch (start us, length us, event | category | flops | bytes accessed | tf_op | source)
XLA Modules:
  0.0 84.2 jit_solution(2183740377599599314)
XLA Ops:
  0.6 1.3 %reshape.18.bias = f32[1,768]{1,0:T(1,128)} reshape(f32[768]{0:T(1024)} %param.10) | data formatting | bytes 6144 | tf_op jit(solution)/shard_map/reshape | solution.py:523
  1.9 77.1 %layer.1 = (bf16[128,384]{1,0:T(8,128)(2,1)}, f32[2,96,768]{2,1,0:T(8,128)}, f32[2,32,768]{2,1,0:T(8,128)}) custom-call(s32[8,8]{1,0:T(8,128)} %table.1, s32[2,2]{1,0:T(2,128)} %counts.1, s32[2,2,8]{2,1,0:T(2,128)} %slots.1, bf16[256,768]{1,0:T(8,128)(2,1)} %feat.1, bf16[256,768]{1,0:T(8,128)(2,1)} %cot.1, f32[1,768]{1,0:T(1,128)} %reshape.18.bias, ...), custom_call_target="tpu_custom_call" | custom-call | tf_op jit(solution)/shard_map/layer/pallas_call | solution.py:468
  79.0 1.0 %copy.13 = bf16[128,384]{0,1:T(8,128)(2,1)S(1)} copy(bf16[128,384]{1,0:T(8,128)(2,1)} %get-tuple-element.6) | data formatting | bytes 196608 | tf_op jit(solution)/shard_map/layer/pallas_call | solution.py:468
  80.0 0.7 copy.17
  80.7 1.9 %copy.20 = f32[2,96,768]{2,1,0:T(8,128)} copy(f32[2,96,768]{2,1,0:T(8,128)} %get-tuple-element.13) | data formatting | bytes 1179648
  82.6 1.6 %copy.21 = f32[2,32,768]{2,1,0:T(8,128)} copy(f32[2,32,768]{2,1,0:T(8,128)} %get-tuple-element.14) | data formatting | bytes 393216

commit v3 on v2

--- a/solution.py
+++ b/solution.py
@@ -32,7 +32,7 @@
     table, counts, slots,
     feat, cot, bias, values_hbm, weights_hbm,
     out, grad_w, grad_f,
-    weights, values, staged, partner_staged, masked, fetched, adj, scale, msg, msg_t, pre,
+    weights, values, staged, partner_staged, masked, fetched, adj, scale, msg, msg_t, wg_own, adj_t, pre,
     pre_send, pre_recv, cot_own, bias_own, gp_all, gp, gm,
     part, part_recv, part_sum, part_back,
     wg_pair, wg_pair_recv, up_send, up_recv, down_send, down_recv,
@@ -135,6 +135,11 @@
         spread(j, 1).wait_recv()
         spread(j, 3).start()
 
+    def arrive(j):
+        fetch(j).wait_recv()
+        spread(j, 0).start()
+        spread(j, 1).start()
+
     load_v.wait()
 
     @pl.loop(0, relations * sections)
@@ -161,19 +166,21 @@
             entry = jnp.zeros((blk, blk), jnp.int32)
             for s in range(slot_total):
                 entry = entry + masked[s] * (slots[r, q, s] == o).astype(jnp.int32)
-            adj[aligned(b * blk, blk, blk), aligned(o * blk, blk, blk)] = entry.astype(F32).astype(BF16)
-
-    @pl.loop(2, n)
-    def _(j):
-        fetch(j).wait_recv()
-        spread(j, 0).start()
-        spread(j, 1).start()
-
-        @pl.when(j > 2)
-        def _():
-            pass_on(j - 1)
-
-    pass_on(n - 1)
+            wide = entry.astype(F32)
+            adj[aligned(b * blk, blk, blk), aligned(o * blk, blk, blk)] = wide.astype(BF16)
+            adj_t[aligned(o * blk, blk, blk), aligned(b * blk, blk, blk)] = wide.T.astype(BF16)
+
+        arrive(b + 2)
+
+    @pl.loop(relations * sections + 2, n)
+    def _(j):
+        arrive(j)
+        pass_on(j - relations * sections)
+
+    @pl.loop(n - relations * sections, n)
+    def _(j):
+        pass_on(j)
+
     load_w.wait()
     fetch_pair.wait_recv()
 
@@ -182,23 +189,24 @@
         spread(j, 2).wait_recv()
         spread(j, 3).wait_recv()
 
-    for r in range(relations):
-        @pl.loop(0, sections)
-        def _(q):
-            at = aligned(r * rows + q * blk, blk, blk)
-            acc = jnp.dot(adj[at, :], fetched[...], preferred_element_type=F32)
-            message = acc * scale[at, 0:1]
-            msg[at, :] = message.astype(BF16)
-
-    @pl.loop(0, sections)
-    def _(q):
+    tile_width = 256
+
+    @pl.loop(0, width // tile_width)
+    def _(c):
+        at = aligned(c * tile_width, tile_width, tile_width)
+        acc = jnp.dot(adj[...], fetched[:, at], preferred_element_type=F32)
+        msg[:, at] = (acc * scale[:, 0:1]).astype(BF16)
+
+    @pl.loop(0, width // tile_width)
+    def _(c):
+        at = aligned(c * tile_width, tile_width, tile_width)
         total = None
         for r in range(relations):
             part_r = jnp.dot(
-                msg[aligned(r * rows + q * blk, blk, blk), :], weights[r], preferred_element_type=F32
+                msg[r * rows : (r + 1) * rows, :], weights[r, :, at], preferred_element_type=F32
             )
             total = part_r if total is None else total + part_r
-        pre[aligned(q * blk, blk, blk), :] = total
+        pre[:, at] = total
 
     whole = pre[...]
     for k in range(groups):
@@ -220,7 +228,9 @@
 
     for r in range(relations):
         turned = msg[r * rows : (r + 1) * rows, :].astype(F32).T
-        msg_t[r] = turned.reshape(n, width // n, rows).astype(BF16)
+        cut = turned.reshape(n, width // n, rows)
+        for c in range(2):
+            msg_t[r, c] = jnp.concatenate([cut[z * 2 + c] for z in range(chips)], axis=0).astype(BF16)
 
     for k in range(groups):
         @pl.when(grp == k)
@@ -260,8 +270,9 @@
             [gp_all[k][:, h * share : (h + 1) * share].astype(F32) for k in range(groups)], axis=1
         ).astype(BF16)
 
-    def weight_chunk(r, t):
-        return jnp.dot(msg_t[r, t], gp[...], preferred_element_type=F32)
+    def weight_chunks(r, c):
+        product = jnp.dot(msg_t[r, c], gp[...], preferred_element_type=F32)
+        return product.reshape(chips, width // n, width)
 
     def pair(z):
         return pltpu.make_async_remote_copy(
@@ -270,11 +281,15 @@
             device_id=(grp, partner), device_id_type=MESH,
         )
 
+    for r in range(relations):
+        wg_pair[:, r] = weight_chunks(r, 1 - core).astype(BF16)
+
     @pl.loop(0, chips)
     def _(z):
-        for r in range(relations):
-            wg_pair[z, r] = weight_chunk(r, z * 2 + 1 - core).astype(BF16)
         pair(z).start()
+
+    for r in range(relations):
+        wg_own[:, r] = weight_chunks(r, core)
 
     def climb(d):
         return pltpu.make_async_remote_copy(
@@ -291,7 +306,7 @@
         )
 
     def chip_sum(r, z):
-        return weight_chunk(r, z * 2 + core) + wg_pair_recv[z, r].astype(F32)
+        return wg_own[z, r] + wg_pair_recv[z, r].astype(F32)
 
     def line_step(step):
         @pl.when(step >= chip)
@@ -334,15 +349,16 @@
 
     line_step(0)
 
-    for r in range(relations):
-        @pl.loop(0, sections)
-        def _(q):
-            at = aligned(r * rows + q * blk, blk, blk)
+    @pl.loop(0, width // tile_width)
+    def _(c):
+        at = aligned(c * tile_width, tile_width, tile_width)
+        for r in range(relations):
+            rows_r = slice(r * rows, (r + 1) * rows)
             grads = lax.dot_general(
-                gp[aligned(q * blk, blk, blk), :], weights[r],
+                gp[...], weights[r, at, :],
                 (((1,), (1,)), ((), ())), preferred_element_type=F32,
             )
-            gm[at, :] = (grads * scale[at, 0:1]).astype(BF16)
+            gm[rows_r, at] = (grads * scale[rows_r, 0:1]).astype(BF16)
 
     def reduce_part(o, i):
         return pltpu.make_async_remote_copy(
@@ -352,16 +368,18 @@
             device_id=(rel(i), me), device_id_type=MESH,
         )
 
-    @pl.loop(0, n)
-    def _(j):
-        o = tgt(j)
-        block = lax.dot_general(
-            adj[:, aligned(o * blk, blk, blk)], gm[...],
-            (((0,), (0,)), ((), ())), preferred_element_type=F32,
-        )
-        part[o] = block.astype(BF16)
-        for i in range(1, groups):
-            reduce_part(o, i).start()
+    batch = 4
+
+    @pl.loop(0, n // batch)
+    def _(e):
+        product = jnp.dot(
+            adj_t[pl.ds(pl.multiple_of(e * batch * blk, blk), batch * blk), :], gm[...],
+            preferred_element_type=F32,
+        )
+        part[pl.ds(e * batch, batch)] = product.reshape(batch, blk, width).astype(BF16)
+        for v in range(batch):
+            for i in range(1, groups):
+                reduce_part(e * batch + v, i).start()
 
     @pl.loop(1, chips - 1)
     def _(step):
@@ -484,7 +502,9 @@
             pltpu.VMEM((relations * rows, n * blk), BF16),
             pltpu.VMEM((relations * rows, 128), F32),
             pltpu.VMEM((relations * rows, width), BF16),
-            pltpu.VMEM((relations, n, chunk, rows), BF16),
+            pltpu.VMEM((relations, 2, chips * chunk, rows), BF16),
+            pltpu.VMEM((chips, relations, chunk, width), F32),
+            pltpu.VMEM((n * blk, relations * rows), BF16),
             pltpu.VMEM((rows, width), F32),
             pltpu.VMEM((groups, half, 2 * share), BF16),
             pltpu.VMEM((groups, half, 2 * share), BF16),

time: 84.5 us -> 83.2 us (0.985)
  Pallas kernels: 77.1 us -> 75.8 us
    pallas_call x1, Pallas kernels: 77.1 us -> 75.8 us  [per_device(): pl.pallas_call(functools.partial(kernel, n, groups), out_shape=(jax.Shape...]
where the time goes in v3:
time: 83.2 us; the launch traced here: 82.9 us
  Pallas kernels  75.8 us (91%)
  local copies, waits for them, and re-layouts  6.47 us (8%)
    pallas_call x1, Pallas kernels, per_device(): pl.pallas_call(functools.partial(kernel, n, groups), out_shape=(jax.Shape...  75.8 us
    unnamed x2, local copies, waits for them, and re-layouts  3.53 us

profile of v3, /device:TPU:0, one launch (start us, length us, event | category | flops | bytes accessed | tf_op | source)
XLA Modules:
  0.0 82.9 jit_solution(7121840878024831784)
XLA Ops:
  0.6 1.3 %reshape.18.bias = f32[1,768]{1,0:T(1,128)} reshape(f32[768]{0:T(1024)} %param.10) | data formatting | bytes 6144 | tf_op jit(solution)/shard_map/reshape | solution.py:543
  1.9 75.8 %layer.1 = (bf16[128,384]{1,0:T(8,128)(2,1)}, f32[2,96,768]{2,1,0:T(8,128)}, f32[2,32,768]{2,1,0:T(8,128)}) custom-call(s32[8,8]{1,0:T(8,128)} %table.1, s32[2,2]{1,0:T(2,128)} %counts.1, s32[2,2,8]{2,1,0:T(2,128)} %slots.1, bf16[256,768]{1,0:T(8,128)(2,1)} %feat.1, bf16[256,768]{1,0:T(8,128)(2,1)} %cot.1, f32[1,768]{1,0:T(1,128)} %reshape.18.bias, ...), custom_call_target="tpu_custom_call" | custom-call | tf_op jit(solution)/shard_map/layer/pallas_call | solution.py:486
  77.7 1.0 %copy.13 = bf16[128,384]{0,1:T(8,128)(2,1)S(1)} copy(bf16[128,384]{1,0:T(8,128)(2,1)} %get-tuple-element.6) | data formatting | bytes 196608 | tf_op jit(solution)/shard_map/layer/pallas_call | solution.py:486
  78.7 0.7 copy.17
  79.4 1.9 %copy.20 = f32[2,96,768]{2,1,0:T(8,128)} copy(f32[2,96,768]{2,1,0:T(8,128)} %get-tuple-element.13) | data formatting | bytes 1179648
  81.3 1.6 %copy.21 = f32[2,32,768]{2,1,0:T(8,128)} copy(f32[2,32,768]{2,1,0:T(8,128)} %get-tuple-element.14) | data formatting | bytes 393216

commit v4 on v3

--- a/solution.py
+++ b/solution.py
@@ -33,7 +33,7 @@
     feat, cot, bias, values_hbm, weights_hbm,
     out, grad_w, grad_f,
     weights, values, staged, partner_staged, masked, fetched, adj, scale, msg, msg_t, wg_own, adj_t, pre,
-    pre_send, pre_recv, cot_own, bias_own, gp_all, gp, gm,
+    pre_send, pre_recv, cot_own, active, bias_own, gp_all, gp, gm,
     part, part_recv, part_sum, part_back,
     wg_pair, wg_pair_recv, up_send, up_recv, down_send, down_recv,
     load_sem, a_send, a_recv, b_send, b_recv, p_send, p_recv, g_send, g_recv,
@@ -236,7 +236,7 @@
         @pl.when(grp == k)
         def _():
             cot_own[...] = pack(cot[...].astype(F32), k * share, share)
-            piece = bias[:, k * share : (k + 1) * share]
+            piece = bias[...].reshape(1, width)[:, k * share : (k + 1) * share]
             bias_own[...] = jnp.concatenate([piece, piece], axis=1)
 
     def gather_gp(i, p):
@@ -259,7 +259,11 @@
         gp_all[grp, at, :] = (cot_own[at, :] * derivative).astype(BF16)
         for i in range(1, groups):
             gather_gp(i, p).start()
-        out[at, :] = (pre_act * sigmoid).astype(BF16)
+        active[at, :] = pre_act * sigmoid
+
+    upright = active[...].T
+    for h in range(2):
+        out[:, h * (rows // 2) : (h + 1) * (rows // 2)] = upright[h * share : (h + 1) * share].astype(BF16)
 
     for p in range(2):
         for i in range(1, groups):
@@ -368,25 +372,17 @@
             device_id=(rel(i), me), device_id_type=MESH,
         )
 
-    batch = 4
-
-    @pl.loop(0, n // batch)
+    @pl.loop(1, chips + 1)
     def _(e):
+        z = lax.rem(chip + e, chips)
         product = jnp.dot(
-            adj_t[pl.ds(pl.multiple_of(e * batch * blk, blk), batch * blk), :], gm[...],
-            preferred_element_type=F32,
-        )
-        part[pl.ds(e * batch, batch)] = product.reshape(batch, blk, width).astype(BF16)
-        for v in range(batch):
+            adj_t[aligned(z * 2 * blk, 2 * blk, blk), :], gm[...], preferred_element_type=F32
+        )
+        for v in range(2):
+            o = z * 2 + v
+            part[o] = product[v * blk : (v + 1) * blk].astype(BF16)
             for i in range(1, groups):
-                reduce_part(e * batch + v, i).start()
-
-    @pl.loop(1, chips - 1)
-    def _(step):
-        line_step(step)
-
-    for r in range(relations):
-        grad_w[r] = chip_sum(r, chip)
+                reduce_part(o, i).start()
 
     def give_back(j):
         return pltpu.make_async_remote_copy(
@@ -402,12 +398,23 @@
             total = total + part_recv[i, o].astype(F32)
         return total.astype(BF16)
 
-    part_back[me] = reduced(me)
-
-    @pl.loop(1, n)
-    def _(j):
+    def send_reduced(j):
         part_sum[tgt(j)] = reduced(tgt(j))
         give_back(j).start()
+
+    @pl.loop(1, chips - 1)
+    def _(step):
+        line_step(step)
+        send_reduced(2 * step)
+        send_reduced(2 * step + 1)
+
+    for r in range(relations):
+        grad_w[r] = chip_sum(r, chip)
+
+    send_reduced(n - 2)
+    send_reduced(n - 1)
+    send_reduced(1)
+    part_back[me] = reduced(me)
 
     @pl.when(chip > 0)
     def _():
@@ -468,6 +475,12 @@
         @pl.when(z < chip)
         def _():
             descend(z).wait_send()
+
+
+def hand_over(out_in, grad_w_in, grad_f_in, out, grad_w, grad_f):
+    out[...] = out_in[...]
+    grad_w[...] = grad_w_in[...]
+    grad_f[...] = grad_f_in[...]
 
 
 def per_device(
@@ -486,7 +499,7 @@
     out, grad_w, grad_f = pl.pallas_call(
         functools.partial(kernel, n, groups),
         out_shape=(
-            jax.ShapeDtypeStruct((half, 2 * share), BF16),
+            jax.ShapeDtypeStruct((share, rows), BF16),
             jax.ShapeDtypeStruct((relations, chunk, width), F32),
             jax.ShapeDtypeStruct((sections, quarter, width), F32),
         ),
@@ -508,6 +521,7 @@
             pltpu.VMEM((rows, width), F32),
             pltpu.VMEM((groups, half, 2 * share), BF16),
             pltpu.VMEM((groups, half, 2 * share), BF16),
+            pltpu.VMEM((half, 2 * share), F32),
             pltpu.VMEM((half, 2 * share), F32),
             pltpu.VMEM((1, 2 * share), F32),
             pltpu.VMEM((groups, half, 2 * share), BF16),
@@ -540,11 +554,18 @@
         name="layer",
     )(
         source_blocks, tile_count, tile_slot,
-        features, cotangent, bias.reshape(1, width),
+        features, cotangent, bias,
         tile_values.reshape(relations, rows * slot_total, blk), weights,
     )
-    output = out.reshape(half, 2, share).swapaxes(0, 1).reshape(rows, share)
-    return (output, grad_w, grad_f)
+    results = (out, grad_w, grad_f)
+    out, grad_w, grad_f = pl.pallas_call(
+        hand_over,
+        out_shape=tuple(jax.ShapeDtypeStruct(x.shape, x.dtype) for x in results),
+        in_specs=[vmem] * 3,
+        out_specs=(vmem,) * 3,
+        name="hand_over",
+    )(*results)
+    return (out.T, grad_w, grad_f)
 
 
 def solution(mesh):

time: 83.2 us -> 78.7 us (0.946)
  local copies, waits for them, and re-layouts: 6.47 us -> 0 us
  Pallas kernels: 75.8 us -> 77.9 us
    unnamed x2 -> x0, local copies, waits for them, and re-layouts: 3.53 us -> none
    pallas_call x0 -> x1, Pallas kernels: none -> 2.08 us  [per_device(): pl.pallas_call(hand_over, out_shape=tuple((jax.ShapeDtypeStruct(x.shape,...]
    reshape x2 -> x0, local copies, waits for them, and re-layouts: 1.93 us -> none  [the longest x1 1.27 us: per_device(): bias.reshape(1, width)]
    pallas_call x1 -> x0, local copies, waits for them, and re-layouts: 1.01 us -> none  [per_device(): pl.pallas_call(functools.partial(kernel, n, groups), out_shape=(jax.Shape...]
where the time goes in v4:
time: 78.7 us; the launch traced here: 78.5 us
  Pallas kernels  77.9 us (99%)
    pallas_call x1, Pallas kernels, per_device(): pl.pallas_call(functools.partial(kernel, n, groups), out_shape=(jax.Shape...  75.8 us
    pallas_call x1, Pallas kernels, per_device(): pl.pallas_call(hand_over, out_shape=tuple((jax.ShapeDtypeStruct(x.shape,...  2.08 us

profile of v4, /device:TPU:0, one launch (start us, length us, event | category | flops | bytes accessed | tf_op | source)
XLA Modules:
  0.0 78.5 jit_solution(8882856847197844765)
XLA Ops:
  0.6 75.8 %layer.1 = (bf16[192,256]{1,0:T(8,128)(2,1)}, f32[2,96,768]{2,1,0:T(8,128)}, f32[2,32,768]{2,1,0:T(8,128)}) custom-call(s32[8,8]{1,0:T(8,128)} %table.1, s32[2,2]{1,0:T(2,128)} %counts.1, s32[2,2,8]{2,1,0:T(2,128)} %slots.1, bf16[256,768]{1,0:T(8,128)(2,1)} %feat.1, bf16[256,768]{1,0:T(8,128)(2,1)} %cot.1, f32[768]{0:T(1024)} %bias.1, ...), custom_call_target="tpu_custom_call" | custom-call | tf_op jit(solution)/shard_map/layer/pallas_call | solution.py:499
  76.5 2.1 %hand_over.1 = (bf16[192,256]{1,0:T(8,128)(2,1)}, f32[2,96,768]{2,1,0:T(8,128)}, f32[2,32,768]{2,1,0:T(8,128)}) custom-call(bf16[192,256]{1,0:T(8,128)(2,1)} %get-tuple-element.9.out_in, f32[2,96,768]{2,1,0:T(8,128)} %get-tuple-element.10.grad_w_in, f32[2,32,768]{2,1,0:T(8,128)} %get-tuple-element.11.grad_f_in), custom_call_target="tpu_custom_call" | custom-call | tf_op jit(solution)/shard_map/hand_over/pallas_call | solution.py:561
